TPU v7x, 32 devices: a whole 2x2x4 slice. The times are simulated.
32 devices in a mesh: frame: 4 (over x, core), fsdp: 4 (over z), head: 2 (over y).
Axes of the slice: x: 2, y: 2, z: 4, core: 2. Of those that a mesh axis runs over, the one named last changes fastest.
Arguments:
- queries: bfloat16 [1024, 10240], P('frame', ('fsdp', 'head')), may hold values from -6 to 6
- noisy_keys: bfloat16 [1024, 10240], P('frame', ('fsdp', 'head')), may hold values from -6 to 6
- noisy_values: bfloat16 [1024, 10240], P('frame', ('fsdp', 'head')), may hold values from -6 to 6
- clean_keys: bfloat16 [1024, 10240], P('frame', ('fsdp', 'head')), may hold values from -10 to 10
- clean_values: bfloat16 [1024, 10240], P('frame', ('fsdp', 'head')), may hold values from -6 to 6
- gain_query: float32 [5120], replicated, may hold values from 0.5 to 2
- gain_key: float32 [5120], replicated, may hold values from 0.5 to 2
- out_grad: bfloat16 [1024, 10240], P('frame', ('fsdp', 'head')), may hold values from -6 to 6
Outputs:
- attended: bfloat16 [1024, 10240], P('frame', ('fsdp', 'head'))
- grad_queries: bfloat16 [1024, 10240], P('frame', ('fsdp', 'head'))
- grad_keys: bfloat16 [1024, 10240], P('frame', ('fsdp', 'head'))
- grad_values: bfloat16 [1024, 10240], P('frame', ('fsdp', 'head'))
- grad_gain_query: float32 [5120], replicated
- grad_gain_key: float32 [5120], replicated
All inputs are finite; a program needn't handle non-finite values.
Results may differ from a plain program's by a relative error of at most 0.012.
Values may be sent and summed in bfloat16 or wider, within the bound.
A program may use at most 64 MiB of HBM per device.

v0:
```python
import math
import jax
import jax.numpy as jnp
from jax import lax
from jax.sharding import PartitionSpec as P

D = 5120
DH = 128
EPSILON = 1e-06
MASKED = -1e30


def shifted(block, axis, distance):
    devices = range(lax.axis_size(axis))
    route = [((i - distance) % len(devices), i) for i in devices]
    return lax.ppermute(block, axis, route)


def project(left_side, right_side):
    return jnp.einsum("qhd,khd->hqk", left_side, right_side, preferred_element_type=jnp.float32)


def on_device(
    queries, noisy_keys, noisy_values, clean_keys, clean_values, gain_query, gain_key, out_grad
):
    length = queries.shape[0]
    width_dev = queries.shape[1]
    head_count = width_dev // DH
    scaling = 1.0 / math.sqrt(DH)
    own_frame = lax.axis_index("frame")
    own_start = own_frame * length
    pair_reach = lax.axis_size("fsdp") // 2
    half_index = lax.axis_index("fsdp") // pair_reach
    column_start = (half_index * lax.axis_size("head") + lax.axis_index("head")) * width_dev
    gain_q = lax.dynamic_slice_in_dim(gain_query, column_start, width_dev)
    gain_k = lax.dynamic_slice_in_dim(gain_key, column_start, width_dev)

    def with_partner(stats):
        other = shifted(stats, "fsdp", pair_reach)
        return stats + other

    q_full = queries.astype(jnp.float32)
    k_full = noisy_keys.astype(jnp.float32)
    squares_q, squares_k = lax.psum(
        (jnp.sum(q_full * q_full, axis=1), jnp.sum(k_full * k_full, axis=1)), "head"
    )
    squares = with_partner(jnp.stack([squares_q, squares_k]))
    rate_q = lax.rsqrt(squares[0] / D + EPSILON)
    rate_k = lax.rsqrt(squares[1] / D + EPSILON)
    normed_q = (
        (q_full * rate_q[:, None] * gain_q).astype(jnp.bfloat16).reshape(length, head_count, DH)
    )
    normed_k = (
        (k_full * rate_k[:, None] * gain_k).astype(jnp.bfloat16).reshape(length, head_count, DH)
    )
    values_own = noisy_values.reshape(length, head_count, DH)
    grads_out = out_grad.reshape(length, head_count, DH)
    own_scores = project(normed_q, normed_k) * scaling
    row_max = jnp.max(own_scores, axis=2)
    expo = jnp.exp(own_scores - row_max[:, :, None])
    totals = jnp.sum(expo, axis=2)
    summed = jnp.einsum(
        "hqk,khd->hqd", expo.astype(jnp.bfloat16), values_own, preferred_element_type=jnp.float32
    )

    def split_piece(portion):
        key_piece, value_piece = portion
        row_count = key_piece.shape[0]
        return (
            key_piece.reshape(row_count, head_count, DH),
            value_piece.reshape(row_count, head_count, DH),
            row_count,
        )

    def visible_scores(key_piece, row_count):
        scores = project(normed_q, key_piece) * scaling
        frame_of = jnp.arange(row_count, dtype=jnp.int32) // length
        return jnp.where((frame_of < own_frame)[None, None, :], scores, MASKED)

    initial = (row_max, totals, summed)
    key_piece, value_piece, row_count = split_piece(
        (
            lax.all_gather(clean_keys, "frame", axis=0, tiled=True),
            lax.all_gather(clean_values, "frame", axis=0, tiled=True),
        )
    )

    def attend(status):
        running, denominator, accumulated = status
        scores = visible_scores(key_piece, row_count)
        newest = jnp.maximum(running, jnp.max(scores, axis=2))
        exponent = jnp.exp(scores - newest[:, :, None])
        factor = jnp.exp(running - newest)
        added = jnp.einsum(
            "hqk,khd->hqd",
            exponent.astype(jnp.bfloat16),
            value_piece,
            preferred_element_type=jnp.float32,
        )
        return (
            newest,
            denominator * factor + jnp.sum(exponent, axis=2),
            accumulated * factor[:, :, None] + added,
        )

    running, denominator, accumulated = lax.cond(
        jnp.int32(0) < own_start, attend, lambda status: status, initial
    )
    log_total = running + jnp.log(denominator)
    output_f32 = accumulated / denominator[:, :, None]
    attended = jnp.transpose(output_f32, (1, 0, 2)).reshape(length, width_dev).astype(jnp.bfloat16)
    delta = jnp.sum(jnp.transpose(grads_out.astype(jnp.float32), (1, 0, 2)) * output_f32, axis=2)
    soft_probs = jnp.exp(own_scores - log_total[:, :, None])
    grad_probs = project(grads_out, values_own)
    grad_scores = (soft_probs * (grad_probs - delta[:, :, None])).astype(jnp.bfloat16)
    grad_qn = (
        jnp.einsum("hqk,khd->qhd", grad_scores, normed_k, preferred_element_type=jnp.float32)
        * scaling
    )
    grad_kn = (
        jnp.einsum("hqk,qhd->khd", grad_scores, normed_q, preferred_element_type=jnp.float32)
        * scaling
    )
    grad_vv = jnp.einsum(
        "hqk,qhd->khd",
        soft_probs.astype(jnp.bfloat16),
        grads_out,
        preferred_element_type=jnp.float32,
    )
    reflect_key_piece, reflect_value_piece, reflect_row_count = split_piece(
        (
            lax.all_gather(clean_keys, "frame", axis=0, tiled=True),
            lax.all_gather(clean_values, "frame", axis=0, tiled=True),
        )
    )

    def attend_back(current):
        scores = visible_scores(reflect_key_piece, reflect_row_count)
        piece_probs = jnp.exp(scores - log_total[:, :, None])
        piece_grads = project(grads_out, reflect_value_piece)
        weighted = (piece_probs * (piece_grads - delta[:, :, None])).astype(jnp.bfloat16)
        return (
            current
            + jnp.einsum(
                "hqk,khd->qhd", weighted, reflect_key_piece, preferred_element_type=jnp.float32
            )
            * scaling
        )

    grad_qn = lax.cond(jnp.int32(0) < own_start, attend_back, lambda current: current, grad_qn)
    plain_q = grad_qn.reshape(length, width_dev)
    plain_k = grad_kn.reshape(length, width_dev)
    flat_q = plain_q * gain_q
    flat_k = plain_k * gain_k
    inner_q, inner_k = lax.psum(
        (jnp.sum(q_full * flat_q, axis=1), jnp.sum(k_full * flat_k, axis=1)), "head"
    )
    inners = with_partner(jnp.stack([inner_q, inner_k]))
    cube_q = rate_q * rate_q * rate_q * inners[0] / D
    cube_k = rate_k * rate_k * rate_k * inners[1] / D
    grad_queries = (rate_q[:, None] * flat_q - q_full * cube_q[:, None]).astype(jnp.bfloat16)
    grad_keys = (rate_k[:, None] * flat_k - k_full * cube_k[:, None]).astype(jnp.bfloat16)
    part_q = jnp.sum(plain_q * q_full * rate_q[:, None], axis=0)
    part_k = jnp.sum(plain_k * k_full * rate_k[:, None], axis=0)
    blank = jnp.zeros((D,), jnp.float32)
    spread_q = lax.dynamic_update_slice_in_dim(blank, part_q, column_start, 0)
    spread_k = lax.dynamic_update_slice_in_dim(blank, part_k, column_start, 0)
    grad_gain_query, grad_gain_key = lax.psum((spread_q, spread_k), ("frame", "fsdp", "head"))
    grad_values = grad_vv.reshape(length, width_dev).astype(jnp.bfloat16)
    return (attended, grad_queries, grad_keys, grad_values, grad_gain_query, grad_gain_key)


def solution(mesh):
    placed = (
        P("frame", ("fsdp", "head")),
        P("frame", ("fsdp", "head")),
        P("frame", ("fsdp", "head")),
        P("frame", ("fsdp", "head")),
        P("frame", ("fsdp", "head")),
        P(),
        P(),
        P("frame", ("fsdp", "head")),
    )
    return jax.shard_map(
        on_device,
        mesh=mesh,
        in_specs=placed,
        out_specs=(
            P("frame", ("fsdp", "head")),
            P("frame", ("fsdp", "head")),
            P("frame", ("fsdp", "head")),
            P("frame", ("fsdp", "head")),
            P(),
            P(),
        ),
        check_vma=False,
    )
```

profile of v0, /device:TPU:0, one launch (start us, length us, event | category | flops | bytes accessed | tf_op | source)
XLA Modules:
  0.0 166.8 jit_solution(3588407405975726999)
XLA Ops:
  7.2 0.0 all-gather.3.cloned.1.call-start
  7.2 0.7 all-gather.3.cloned.1.call-update
  7.9 0.0 all-gather.5.cloned.1.call-start
  8.0 2.2 %copy.46 = bf16[256,1280]{0,1:T(8,128)(2,1)} copy(bf16[256,1280]{1,0:T(8,128)(2,1)} %param.16) | data formatting | bytes 1310720 | tf_op args[4]
  10.1 0.0 all-gather.5.cloned.1.call-update
  10.2 0.0 copy-start.20
  10.2 0.2 copy.38
  10.4 0.2 copy.39
  10.7 0.2 fusion.38
  10.9 0.2 fusion.46
  11.1 5.9 %all-reduce.2 = (f32[1,256]{1,0:T(1,128)S(1)}, f32[1,256]{1,0:T(1,128)S(1)}) all-reduce(f32[1,256]{1,0:T(1,128)S(1)} %bitcast.86, f32[1,256]{1,0:T(1,128)S(1)} %bitcast.85), channel_id=1, replica_groups=mesh['frame'=4,'fsdp'=4,'head'=2] {'head'}, use_global_device_ids=true, to_apply=%region_3.4 | all-reduce | flops 512 | bytes 4096 | tf_op jit(solution)/shard_map/psum | solution.py:44
  17.0 3.2 %collective-permute-start = (f32[2,256]{1,0:T(2,128)S(1)}, f32[2,256]{1,0:T(2,128)S(1)}, u32[]{:S(2)}, u32[]{:S(2)}) collective-permute-start(f32[2,256]{1,0:T(2,128)S(1)} %pad_maximum_fusion), channel_id=1, source_target_pairs={{4,0},{6,2},{0,4},{2,6},{5,1},{7,3},{1,5},{3,7},{12,8},{14,10},{8,... | collective-permute-start | bytes 6152 | tf_op jit(solution)/shard_map/ppermute | solution.py:16
  20.2 0.8 dynamic_slice.6
  20.9 0.8 dynamic_slice.7
  21.7 1.1 copy.42
  22.8 1.1 copy.51
  23.9 0.2 fusion.40
  24.2 0.2 fusion.48
  24.4 0.0 copy-start.9
  24.4 0.6 multiply_reduce_fusion
  25.0 0.3 copy-done.11
  25.3 0.4 fusion.32
  25.8 0.0 copy-done.9
  25.8 1.8 %fusion.36 = f32[10,256,128]{2,1,0:T(8,128)} fusion(bf16[256,10,128]{0,2,1:T(8,128)(2,1)S(1)} %bitcast.69, f32[10,256,256]{1,2,0:T(8,128)S(1)} %get-tuple-element.167, f32[10,256]{1,0:T(8,128)S(1)} %get-tuple-element.166), kind=kOutput, calls=%fused_computation.61 | convolution fusion | flops 169738240 | bytes 4597760 | tf_op jit(solution)/shard_map/hqk,khd->hqd/dot_general | solution.py:62
  27.6 10.3 %all-gather.3.cloned.1.call-done = bf16[1024,1280]{1,0:T(8,128)(2,1)} async-done(((bf16[256,1280]{1,0:T(8,128)(2,1)}), bf16[1024,1280]{1,0:T(8,128)(2,1)}) %all-gather.3.cloned.1.call-update) | async-done | bytes 2621456 | tf_op jit(solution)/shard_map/all_gather | solution.py:83
  37.9 4.5 %copy.45 = bf16[1024,1280]{0,1:T(8,128)(2,1)} copy(bf16[1024,1280]{1,0:T(8,128)(2,1)} %all-gather.3.cloned.1.call-done) | data formatting | bytes 5242880 | tf_op jit(solution)/shard_map/all_gather | solution.py:83
  42.4 23.5 %all-gather.5.cloned.1.call-done = bf16[1024,1280]{0,1:T(8,128)(2,1)} async-done(((bf16[256,1280]{0,1:T(8,128)(2,1)}), bf16[1024,1280]{0,1:T(8,128)(2,1)}) %all-gather.5.cloned.1.call-update) | async-done | bytes 2621456 | tf_op jit(solution)/shard_map/all_gather | solution.py:84
  65.9 2.8 %copy.50 = f32[10,256,128]{1,2,0:T(8,128)} copy(f32[10,256,128]{2,1,0:T(8,128)} %get-tuple-element.144) | data formatting | bytes 2621440 | tf_op jit(solution)/shard_map/cond | solution.py:106
  68.7 2.7 %convolution_convert_fusion = bf16[10,256,128]{1,2,0:T(8,128)(2,1)} fusion(bf16[256,10,128]{0,2,1:T(8,128)(2,1)} %bitcast.65, f32[10,256,256]{1,2,0:T(8,128)S(1)} %get-tuple-element.167, f32[10,256]{1,0:T(8,128)S(1)} %log_add_fusion), kind=kOutput, calls=%fused_computation.60 | convolution fusion | flops 170065920 | bytes 3942400 | tf_op jit(solution)/shard_map/hqk,qhd->khd/dot_general | solution.py:124
  71.5 1.1 fusion.54
  72.5 0.8 multiply_convert_fusion.8
  73.3 0.3 copy-done.12
  73.6 1.4 fusion.34
  75.0 0.6 convolution_multiply_fusion
  75.6 0.7 fusion.53
  76.3 0.9 copy-done
  77.3 2.1 %fusion.45 = (f32[1280]{0:T(1024)S(1)}, f32[256]{0:T(256)S(1)}) fusion(f32[256,1280]{0,1:T(8,128)} %get-tuple-element.92, bf16[256,1280]{0,1:T(8,128)(2,1)S(1)} %copy.38, f32[256]{0:T(256)S(1)} %bitcast.76, f32[1280]{0:T(1024)S(1)} %dynamic_slice.6), kind=kLoop, calls=%fused_computation.69 | loop fusion | flops 2292224 | bytes 1978368 | tf_op jit(solution)/shard_map/reduce_sum | solution.py:163
  79.4 4.9 %all-reduce.1 = (f32[1,256]{1,0:T(1,128)S(1)}, f32[1,256]{1,0:T(1,128)S(1)}) all-reduce(f32[1,256]{1,0:T(1,128)S(1)} %bitcast.83, f32[1,256]{1,0:T(1,128)S(1)} %bitcast.84), channel_id=1, replica_groups=mesh['frame'=4,'fsdp'=4,'head'=2] {'head'}, use_global_device_ids=true, to_apply=%region_16.17 | all-reduce | flops 512 | bytes 4096 | tf_op jit(solution)/shard_map/psum | solution.py:155
  84.3 2.5 %collective-permute-start.1 = (f32[2,256]{1,0:T(2,128)S(1)}, f32[2,256]{1,0:T(2,128)S(1)}, u32[]{:S(2)}, u32[]{:S(2)}) collective-permute-start(f32[2,256]{1,0:T(2,128)S(1)} %pad_maximum_fusion.1), channel_id=1, source_target_pairs={{4,0},{6,2},{0,4},{2,6},{5,1},{7,3},{1,5},{3,7},{12,8},{14,10},{8,... | collective-permute-start | bytes 6152 | tf_op jit(solution)/shard_map/ppermute | solution.py:16
  86.8 0.2 dynamic_update_slice.7
  87.0 0.3 dynamic_update_slice.6
  87.3 65.2 %all-reduce = (f32[5120]{0:T(1024)}, f32[5120]{0:T(1024)}) all-reduce(f32[5120]{0:T(1024)S(1)} %dynamic_update_slice.6, f32[5120]{0:T(1024)S(1)} %dynamic_update_slice.7), channel_id=1, replica_groups=mesh['frame'=4,'fsdp'=4,'head'=2] {'frame','fsdp','head'}, use_global_device_ids=true, to_apply=%region_18.19 | all-reduce | flops 10240 | bytes 81920 | tf_op jit(solution)/shard_map/psum | solution.py:168
  152.6 2.2 %copy.64 = bf16[256,1280]{1,0:T(8,128)(2,1)} copy(bf16[256,1280]{0,1:T(8,128)(2,1)} %bitcast.74) | data formatting | bytes 1310720
  154.8 1.1 copy.61
  155.9 0.3 fusion.51
  156.2 1.1 copy.63
  157.3 1.6 fusion.43
  158.9 1.1 copy.62
  (47 shorter events, 0.2 us)
Async XLA Ops:
  7.2 3.0 %copy-start.17 = (bf16[256,1280]{1,0:T(8,128)(2,1)S(1)}, bf16[256,1280]{1,0:T(8,128)(2,1)}, u32[]{:S(2)}) copy-start(bf16[256,1280]{1,0:T(8,128)(2,1)} %param.12) | copy-start | bytes 1966084
  7.2 3.2 %copy-start.18 = (bf16[256,1280]{1,0:T(8,128)(2,1)S(1)}, bf16[256,1280]{1,0:T(8,128)(2,1)}, u32[]{:S(2)}) copy-start(bf16[256,1280]{1,0:T(8,128)(2,1)} %param.13) | copy-start | bytes 1966084
  7.2 30.7 %all-gather.3.cloned.1.call-start = ((), (), s32[]{:S(2)}) async-start(), calls=%async_computation | async-start | bytes 3276800 | tf_op jit(solution)/shard_map/all_gather | solution.py:83
  7.9 58.0 %all-gather.5.cloned.1.call-start = ((), (), s32[]{:S(2)}) async-start(), calls=%async_computation.1 | async-start | bytes 3276800 | tf_op jit(solution)/shard_map/all_gather | solution.py:84
  10.1 11.6 %copy-start.19 = (bf16[256,1280]{1,0:T(8,128)(2,1)S(1)}, bf16[256,1280]{1,0:T(8,128)(2,1)}, u32[]{:S(2)}) copy-start(bf16[256,1280]{1,0:T(8,128)(2,1)} %param.14) | copy-start | bytes 1966084
  10.2 12.6 %copy-start.20 = (bf16[256,1280]{1,0:T(8,128)(2,1)S(1)}, bf16[256,1280]{1,0:T(8,128)(2,1)}, u32[]{:S(2)}) copy-start(bf16[256,1280]{1,0:T(8,128)(2,1)} %param.19) | copy-start | bytes 1966084
  10.7 13.5 %copy-start.1 = (bf16[256,1280]{0,1:T(8,128)(2,1)}, bf16[256,1280]{0,1:T(8,128)(2,1)S(1)}, u32[]{:S(2)}) copy-start(bf16[256,1280]{0,1:T(8,128)(2,1)S(1)} %copy.39) | copy-start | bytes 1966084
  17.0 6.9 %collective-permute-start = (f32[2,256]{1,0:T(2,128)S(1)}, f32[2,256]{1,0:T(2,128)S(1)}, u32[]{:S(2)}, u32[]{:S(2)}) collective-permute-start(f32[2,256]{1,0:T(2,128)S(1)} %pad_maximum_fusion), channel_id=1, source_target_pairs={{4,0},{6,2},{0,4},{2,6},{5,1},{7,3},{1,5},{3,7},{12,8},{14,10},{8,... | collective-permute-start | bytes 6152 | tf_op jit(solution)/shard_map/ppermute | solution.py:16
  24.2 0.9 copy-start.4
  24.4 0.9 copy-start.11
  24.4 1.4 copy-start.9
  68.7 2.8 %copy-start.8 = (bf16[256,1280]{0,1:T(8,128)(2,1)S(1)}, bf16[256,1280]{0,1:T(8,128)(2,1)}, u32[]{:S(2)}) copy-start(bf16[256,1280]{0,1:T(8,128)(2,1)} %copy.51) | copy-start | bytes 1966084
  68.7 2.8 %copy-start.13 = (f32[10,256,128]{1,2,0:T(8,128)S(1)}, f32[10,256,128]{1,2,0:T(8,128)}, u32[]{:S(2)}) copy-start(f32[10,256,128]{1,2,0:T(8,128)} %copy.50) | copy-start | bytes 3932164
  68.7 3.8 %copy-start.10 = (bf16[256,1280]{0,1:T(8,128)(2,1)S(1)}, bf16[256,1280]{0,1:T(8,128)(2,1)}, u32[]{:S(2)}) copy-start(bf16[256,1280]{0,1:T(8,128)(2,1)} %copy.42) | copy-start | bytes 1966084
  72.5 1.1 copy-start.12
  73.6 1.4 copy-start.5
  73.6 2.0 %copy-start.2 = (bf16[256,1280]{0,1:T(8,128)(2,1)S(1)}, bf16[256,1280]{0,1:T(8,128)(2,1)}, u32[]{:S(2)}) copy-start(bf16[256,1280]{0,1:T(8,128)(2,1)} %copy-done.1) | copy-start | bytes 1966084
  75.0 2.2 %copy-start = (bf16[1024,1280]{0,1:T(8,128)(2,1)S(1)}, bf16[1024,1280]{0,1:T(8,128)(2,1)}, u32[]{:S(2)}) copy-start(bf16[1024,1280]{0,1:T(8,128)(2,1)} %copy.45) | copy-start | bytes 7864324
  75.6 1.6 copy-start.6
  77.3 77.5 %copy-start.16 = (bf16[10,256,128]{1,2,0:T(8,128)(2,1)S(1)}, bf16[10,256,128]{1,2,0:T(8,128)(2,1)}, u32[]{:S(2)}) copy-start(bf16[10,256,128]{1,2,0:T(8,128)(2,1)} %get-tuple-element.161) | copy-start | bytes 1966084
  77.3 78.6 %copy-start.3 = (bf16[256,1280]{0,1:T(8,128)(2,1)S(1)}, bf16[256,1280]{0,1:T(8,128)(2,1)}, u32[]{:S(2)}) copy-start(bf16[256,1280]{0,1:T(8,128)(2,1)} %copy-done.1) | copy-start | bytes 1966084
  77.3 78.6 %copy-start.7 = (f32[10,128,256]{2,1,0:T(8,128)S(1)}, f32[10,128,256]{2,1,0:T(8,128)}, u32[]{:S(2)}) copy-start(f32[10,128,256]{2,1,0:T(8,128)} %copy-done.6) | copy-start | bytes 3932164
  84.3 71.5 %collective-permute-start.1 = (f32[2,256]{1,0:T(2,128)S(1)}, f32[2,256]{1,0:T(2,128)S(1)}, u32[]{:S(2)}, u32[]{:S(2)}) collective-permute-start(f32[2,256]{1,0:T(2,128)S(1)} %pad_maximum_fusion.1), channel_id=1, source_target_pairs={{4,0},{6,2},{0,4},{2,6},{5,1},{7,3},{1,5},{3,7},{12,8},{14,10},{8,... | collective-permute-start | bytes 6152 | tf_op jit(solution)/shard_map/ppermute | solution.py:16
Sparse Core Ops, SparseCore 0:
  9.6 28.2 all-gather.2
  40.0 25.8 all-gather.4
where the time goes:
time: 167 us
  blocking collectives  76.1 us (46%)
  waiting for transfers between devices  34.5 us (21%)
  local copies, waits for them, and re-layouts  21.2 us (13%)
  between operations  14.3 us (9%)
  matrix products  7.9 us (5%)
  other arithmetic  7.13 us (4%)
  starting transfers between devices  5.7 us (3%)
    psum x1, blocking collectives, on_device(): lax.psum((spread_q, spread_k), ('frame', 'fsdp', 'head'))  65.2 us
    all_gather x1, waiting for transfers between devices, on_device(): lax.all_gather(clean_values, 'frame', axis=0, tiled=True)  23.5 us
    unnamed x47, local copies, waits for them, and re-layouts  11.8 us
    all_gather x1, waiting for transfers between devices, on_device(): lax.all_gather(clean_keys, 'frame', axis=0, tiled=True)  10.3 us
    psum x1, blocking collectives, on_device(): lax.psum((jnp.sum(q_full * q_full, axis=1), jnp.sum(k_full * k_full, axis...  5.89 us
    ppermute x2, starting transfers between devices, shifted(): return lax.ppermute(block, axis, route)  5.62 us
    psum x1, blocking collectives, on_device(): lax.psum((jnp.sum(q_full * flat_q, axis=1), jnp.sum(k_full * flat_k, axis...  4.93 us
    all_gather x1, local copies, waits for them, and re-layouts, on_device(): lax.all_gather(clean_keys, 'frame', axis=0, tiled=True)  4.54 us
  transfers between devices with their start and end apart: 4, of which 2 were waited for; matrix products, arithmetic and copies ran while one was open for 11% of the time, Pallas kernels for 0%

commit v1 on v0

--- a/solution.py
+++ b/solution.py
@@ -78,11 +78,33 @@
         return jnp.where((frame_of < own_frame)[None, None, :], scores, MASKED)
 
     initial = (row_max, totals, summed)
+
+    def rings_pair(q_in, dim_k):
+        r_now = jax.lax.axis_index("frame")
+        z = jax.lax.axis_size("frame")
+        front, then, even = (z, r_now, q_in.shape[dim_k])
+        blocks_here = [j0 * front if j == dim_k else j0 for j, j0 in enumerate(q_in.shape)]
+        lower = jnp.zeros(blocks_here, q_in.dtype)
+        moved = lax.dynamic_update_slice_in_dim(lower, q_in, then * even, axis=dim_k)
+        carry_out = right_arr = q_in
+        for w in range(1, front // 2 + 1):
+            base_arr = map(lambda j: (j, (j + 1) % front), range(front))
+            arr_now = list(base_arr)
+            carry_out = jax.lax.ppermute(carry_out, "frame", arr_now)
+            moved = lax.dynamic_update_slice_in_dim(
+                moved, carry_out, (then - w) % front * even, axis=dim_k
+            )
+            if 2 * w < front:
+                tall = map(lambda j: (j, (j - 1) % front), range(front))
+                y_new = list(tall)
+                right_arr = jax.lax.ppermute(right_arr, "frame", perm=y_new)
+                moved = lax.dynamic_update_slice_in_dim(
+                    moved, right_arr, (then + w) % front * even, axis=dim_k
+                )
+        return moved
+
     key_piece, value_piece, row_count = split_piece(
-        (
-            lax.all_gather(clean_keys, "frame", axis=0, tiled=True),
-            lax.all_gather(clean_values, "frame", axis=0, tiled=True),
-        )
+        (lax.all_gather(clean_keys, "frame", axis=0, tiled=True), rings_pair(clean_values, 0))
     )
 
     def attend(status):

time: 167 us -> 175 us (1.048)
  waiting for transfers between devices: 34.5 us -> 23.7 us
  starting transfers between devices: 5.7 us -> 15.2 us
  blocking collectives: 76.1 us -> 82.1 us
  other arithmetic: 7.13 us -> 10 us
    all_gather x1, waiting for transfers between devices: 23.5 us -> 12.2 us  [on_device(): lax.all_gather(clean_values, 'frame', axis=0, tiled=True)]
    ppermute x0 -> x3, starting transfers between devices: none -> 9.51 us  [the longest x2 7.59 us: rings_pair(): carry_out = jax.lax.ppermute(carry_out, 'frame', arr_now)]
    psum x1, blocking collectives: 65.2 us -> 71.9 us  [on_device(): lax.psum((spread_q, spread_k), ('frame', 'fsdp', 'head'))]
    unnamed x47 -> x37, local copies, waits for them, and re-layouts: 11.8 us -> 11.7 us
  transfers between devices with their start and end apart: 4 -> 7, of which waited for: 2 -> 3; matrix products, arithmetic and copies ran while one was open for 11% -> 17% of each run, Pallas kernels for 0% -> 0%
where the time goes in v1:
time: 175 us; the launch traced here: 174 us
  blocking collectives  82.1 us (47%)
  waiting for transfers between devices  23.7 us (14%)
  local copies, waits for them, and re-layouts  21.1 us (12%)
  starting transfers between devices  15.2 us (9%)
  between operations  14.3 us (8%)
  other arithmetic  10 us (6%)
  matrix products  7.69 us (4%)
    psum x1, blocking collectives, on_device(): lax.psum((spread_q, spread_k), ('frame', 'fsdp', 'head'))  71.9 us
    all_gather x1, waiting for transfers between devices, on_device(): lax.all_gather(clean_values, 'frame', axis=0, tiled=True)  12.2 us
    unnamed x37, local copies, waits for them, and re-layouts  11.7 us
    all_gather x1, waiting for transfers between devices, on_device(): lax.all_gather(clean_keys, 'frame', axis=0, tiled=True)  9.34 us
    ppermute x2, starting transfers between devices, rings_pair(): carry_out = jax.lax.ppermute(carry_out, 'frame', arr_now)  7.59 us
    ppermute x2, starting transfers between devices, shifted(): return lax.ppermute(block, axis, route)  5.62 us
    psum x1, blocking collectives, on_device(): lax.psum((jnp.sum(q_full * q_full, axis=1), jnp.sum(k_full * k_full, axis...  5.23 us
    psum x1, blocking collectives, on_device(): lax.psum((jnp.sum(q_full * flat_q, axis=1), jnp.sum(k_full * flat_k, axis...  4.93 us
  transfers between devices with their start and end apart: 7, of which 3 were waited for; matrix products, arithmetic and copies ran while one was open for 17% of the time, Pallas kernels for 0%

profile of v1, /device:TPU:0, one launch (start us, length us, event | category | flops | bytes accessed | tf_op | source)
XLA Modules:
  0.0 174.2 jit_solution(7409436228303800966)
XLA Ops:
  7.2 0.0 all-gather.3.cloned.1.call-start
  7.2 0.7 all-gather.3.cloned.1.call-update
  7.9 0.0 all-gather.5.cloned.1.call-start
  8.0 2.2 %copy.46 = bf16[256,1280]{0,1:T(8,128)(2,1)} copy(bf16[256,1280]{1,0:T(8,128)(2,1)} %param.16) | data formatting | bytes 1310720 | tf_op args[4]
  10.1 0.5 collective-permute-start.1
  10.6 1.9 %collective-permute-start.2 = (bf16[256,1280]{0,1:T(8,128)(2,1)}, bf16[256,1280]{0,1:T(8,128)(2,1)}, u32[]{:S(2)}, u32[]{:S(2)}) collective-permute-start(bf16[256,1280]{0,1:T(8,128)(2,1)} %copy.46), channel_id=1, source_target_pairs={{0,24},{8,0},{16,8},{24,16},{1,25},{9,1},{17,9},{25,17},{2,26},{10... | collective-permute-start | bytes 1966088 | tf_op jit(solution)/shard_map/ppermute | solution.py:100
  12.5 1.3 copy.38
  13.9 0.2 copy.39
  14.1 0.2 fusion.38
  14.3 0.2 fusion.46
  14.5 5.2 %all-reduce.2 = (f32[1,256]{1,0:T(1,128)S(1)}, f32[1,256]{1,0:T(1,128)S(1)}) all-reduce(f32[1,256]{1,0:T(1,128)S(1)} %bitcast.90, f32[1,256]{1,0:T(1,128)S(1)} %bitcast.89), channel_id=1, replica_groups=mesh['frame'=4,'fsdp'=4,'head'=2] {'head'}, use_global_device_ids=true, to_apply=%region_3.4 | all-reduce | flops 512 | bytes 4096 | tf_op jit(solution)/shard_map/psum | solution.py:44
  19.8 3.2 %collective-permute-start = (f32[2,256]{1,0:T(2,128)S(1)}, f32[2,256]{1,0:T(2,128)S(1)}, u32[]{:S(2)}, u32[]{:S(2)}) collective-permute-start(f32[2,256]{1,0:T(2,128)S(1)} %pad_maximum_fusion), channel_id=1, source_target_pairs={{4,0},{6,2},{0,4},{2,6},{5,1},{7,3},{1,5},{3,7},{12,8},{14,10},{8,... | collective-permute-start | bytes 6152 | tf_op jit(solution)/shard_map/ppermute | solution.py:16
  23.0 0.8 dynamic_slice.7
  23.8 0.8 dynamic_slice.6
  24.6 1.1 copy.42
  25.6 1.1 copy.52
  26.8 0.2 fusion.48
  27.0 0.2 fusion.40
  27.3 1.4 collective-permute-done.1
  28.7 7.1 %collective-permute-start.3 = (bf16[256,1280]{0,1:T(8,128)(2,1)}, bf16[256,1280]{0,1:T(8,128)(2,1)}, u32[]{:S(2)}, u32[]{:S(2)}) collective-permute-start(bf16[256,1280]{0,1:T(8,128)(2,1)} %collective-permute-done.1), channel_id=1, source_target_pairs={{0,8},{8,16},{16,24},{24,0},{1,9},{9,17},{17,25},{25,1},{2,10},{10... | collective-permute-start | bytes 1966088 | tf_op jit(solution)/shard_map/ppermute | solution.py:93
  35.8 0.6 multiply_reduce_fusion
  36.4 0.4 fusion.32
  36.8 0.1 copy-done.7
  36.9 1.8 %fusion.36 = f32[10,256,128]{2,1,0:T(8,128)} fusion(bf16[256,10,128]{0,2,1:T(8,128)(2,1)S(1)} %bitcast.72, f32[10,256,256]{1,2,0:T(8,128)S(1)} %get-tuple-element.444, f32[10,256]{1,0:T(8,128)S(1)} %get-tuple-element.443), kind=kOutput, calls=%fused_computation.64 | convolution fusion | flops 169738240 | bytes 4597760 | tf_op jit(solution)/shard_map/hqk,khd->hqd/dot_general | solution.py:62
  38.7 9.3 %all-gather.3.cloned.1.call-done = bf16[1024,1280]{1,0:T(8,128)(2,1)} async-done(((bf16[256,1280]{1,0:T(8,128)(2,1)}), bf16[1024,1280]{1,0:T(8,128)(2,1)}) %all-gather.3.cloned.1.call-update) | async-done | bytes 2621456 | tf_op jit(solution)/shard_map/all_gather | solution.py:107
  48.0 4.5 %copy.45 = bf16[1024,1280]{0,1:T(8,128)(2,1)} copy(bf16[1024,1280]{1,0:T(8,128)(2,1)} %all-gather.3.cloned.1.call-done) | data formatting | bytes 5242880 | tf_op jit(solution)/shard_map/all_gather | solution.py:107
  52.5 0.2 conditional.2
  52.7 2.8 %copy.51 = f32[10,256,128]{1,2,0:T(8,128)} copy(f32[10,256,128]{2,1,0:T(8,128)} %get-tuple-element.421) | data formatting | bytes 2621440 | tf_op jit(solution)/shard_map/cond | solution.py:128
  55.5 2.8 %fusion.54 = (f32[10,256]{1,0:T(8,128)S(1)}, bf16[10,256,128]{1,2,0:T(8,128)(2,1)}) fusion(bf16[256,10,128]{0,2,1:T(8,128)(2,1)} %bitcast.68, f32[10,256,128]{1,2,0:T(8,128)} %copy.51, f32[10,256]{1,0:T(8,128)S(1)} %get-tuple-element.420), kind=kLoop, calls=%fused_computation.83 | loop fusion | flops 1635840 | bytes 2641920 | tf_op jit(solution)/shard_map/reduce_sum | solution.py:134
  58.3 0.8 multiply_convert_fusion.8
  59.1 0.3 copy-done.10
  59.4 1.4 fusion.34
  60.8 1.6 convolution_multiply_fusion
  62.4 1.5 convolution_convert_fusion
  63.9 12.2 %all-gather.5.cloned.1.call-done = bf16[1024,1280]{0,1:T(8,128)(2,1)} async-done(((bf16[256,1280]{0,1:T(8,128)(2,1)}), bf16[1024,1280]{0,1:T(8,128)(2,1)}) %all-gather.5.cloned.1.call-update) | async-done | bytes 2621456 | tf_op jit(solution)/shard_map/all_gather | solution.py:155
  76.2 2.1 %fusion.45 = (f32[1280]{0:T(1024)S(1)}, f32[256]{0:T(256)S(1)}) fusion(f32[256,1280]{0,1:T(8,128)} %get-tuple-element.330, bf16[256,1280]{0,1:T(8,128)(2,1)S(1)} %copy.38, f32[256]{0:T(256)S(1)} %bitcast.80, f32[1280]{0:T(1024)S(1)} %dynamic_slice.6), kind=kLoop, calls=%fused_computation.72 | loop fusion | flops 2292224 | bytes 1978368 | tf_op jit(solution)/shard_map/reduce_sum | solution.py:185
  78.3 1.8 %fusion.53 = (f32[1280]{0:T(1024)S(1)}, f32[256]{0:T(256)S(1)}) fusion(bf16[256,1280]{0,1:T(8,128)(2,1)} %copy-done.1, f32[10,128,256]{2,1,0:T(8,128)S(1)} %copy-done.5, f32[256]{0:T(256)S(1)} %bitcast.84, f32[1280]{0:T(1024)S(1)} %dynamic_slice.7), kind=kLoop, calls=%fused_computation.80 | loop fusion | flops 2292224 | bytes 1978368 | tf_op jit(solution)/shard_map/reduce_sum | solution.py:186
  80.2 4.9 %all-reduce.1 = (f32[1,256]{1,0:T(1,128)S(1)}, f32[1,256]{1,0:T(1,128)S(1)}) all-reduce(f32[1,256]{1,0:T(1,128)S(1)} %bitcast.88, f32[1,256]{1,0:T(1,128)S(1)} %bitcast.87), channel_id=1, replica_groups=mesh['frame'=4,'fsdp'=4,'head'=2] {'head'}, use_global_device_ids=true, to_apply=%region_16.17 | all-reduce | flops 512 | bytes 4096 | tf_op jit(solution)/shard_map/psum | solution.py:177
  85.1 2.5 %collective-permute-start.4 = (f32[2,256]{1,0:T(2,128)S(1)}, f32[2,256]{1,0:T(2,128)S(1)}, u32[]{:S(2)}, u32[]{:S(2)}) collective-permute-start(f32[2,256]{1,0:T(2,128)S(1)} %pad_maximum_fusion.1), channel_id=1, source_target_pairs={{4,0},{6,2},{0,4},{2,6},{5,1},{7,3},{1,5},{3,7},{12,8},{14,10},{8,... | collective-permute-start | bytes 6152 | tf_op jit(solution)/shard_map/ppermute | solution.py:16
  87.6 0.2 dynamic_update_slice.38
  87.8 0.3 dynamic_update_slice.39
  88.1 71.9 %all-reduce = (f32[5120]{0:T(1024)}, f32[5120]{0:T(1024)}) all-reduce(f32[5120]{0:T(1024)S(1)} %dynamic_update_slice.38, f32[5120]{0:T(1024)S(1)} %dynamic_update_slice.39), channel_id=1, replica_groups=mesh['frame'=4,'fsdp'=4,'head'=2] {'frame','fsdp','head'}, use_global_device_ids=true, to_apply=%region_18.19 | all-reduce | flops 10240 | bytes 81920 | tf_op jit(solution)/shard_map/psum | solution.py:190
  160.0 2.2 %copy.65 = bf16[256,1280]{1,0:T(8,128)(2,1)} copy(bf16[256,1280]{0,1:T(8,128)(2,1)} %bitcast.78) | data formatting | bytes 1310720
  162.2 1.1 copy.62
  163.3 0.3 fusion.51
  163.6 1.1 copy.64
  164.7 1.6 fusion.43
  166.3 1.1 copy.63
  (43 shorter events, 0.2 us)
Async XLA Ops:
  7.2 6.7 %copy-start.15 = (bf16[256,1280]{1,0:T(8,128)(2,1)S(1)}, bf16[256,1280]{1,0:T(8,128)(2,1)}, u32[]{:S(2)}) copy-start(bf16[256,1280]{1,0:T(8,128)(2,1)} %param.13) | copy-start | bytes 1966084
  7.2 40.8 %all-gather.3.cloned.1.call-start = ((), (), s32[]{:S(2)}) async-start(), calls=%async_computation | async-start | bytes 3276800 | tf_op jit(solution)/shard_map/all_gather | solution.py:107
  7.9 68.3 %all-gather.5.cloned.1.call-start = ((), (), s32[]{:S(2)}) async-start(), calls=%async_computation.1 | async-start | bytes 3276800 | tf_op jit(solution)/shard_map/all_gather | solution.py:155
  10.1 14.4 %copy-start.16 = (bf16[256,1280]{1,0:T(8,128)(2,1)S(1)}, bf16[256,1280]{1,0:T(8,128)(2,1)}, u32[]{:S(2)}) copy-start(bf16[256,1280]{1,0:T(8,128)(2,1)} %param.14) | copy-start | bytes 1966084
  10.1 18.5 %collective-permute-start.1 = (bf16[256,1280]{0,1:T(8,128)(2,1)}, bf16[256,1280]{0,1:T(8,128)(2,1)}, u32[]{:S(2)}, u32[]{:S(2)}) collective-permute-start(bf16[256,1280]{0,1:T(8,128)(2,1)} %copy.46), channel_id=1, source_target_pairs={{0,8},{8,16},{16,24},{24,0},{1,9},{9,17},{17,25},{25,1},{2,10},{10... | collective-permute-start | bytes 1966088 | tf_op jit(solution)/shard_map/ppermute | solution.py:93
  10.6 41.9 %collective-permute-start.2 = (bf16[256,1280]{0,1:T(8,128)(2,1)}, bf16[256,1280]{0,1:T(8,128)(2,1)}, u32[]{:S(2)}, u32[]{:S(2)}) collective-permute-start(bf16[256,1280]{0,1:T(8,128)(2,1)} %copy.46), channel_id=1, source_target_pairs={{0,24},{8,0},{16,8},{24,16},{1,25},{9,1},{17,9},{25,17},{2,26},{10... | collective-permute-start | bytes 1966088 | tf_op jit(solution)/shard_map/ppermute | solution.py:100
  13.9 11.8 %copy-start.17 = (bf16[256,1280]{1,0:T(8,128)(2,1)S(1)}, bf16[256,1280]{1,0:T(8,128)(2,1)}, u32[]{:S(2)}) copy-start(bf16[256,1280]{1,0:T(8,128)(2,1)} %param.19) | copy-start | bytes 1966084
  14.1 12.9 %copy-start.1 = (bf16[256,1280]{0,1:T(8,128)(2,1)}, bf16[256,1280]{0,1:T(8,128)(2,1)S(1)}, u32[]{:S(2)}) copy-start(bf16[256,1280]{0,1:T(8,128)(2,1)S(1)} %copy.39) | copy-start | bytes 1966084
  19.8 6.9 %collective-permute-start = (f32[2,256]{1,0:T(2,128)S(1)}, f32[2,256]{1,0:T(2,128)S(1)}, u32[]{:S(2)}, u32[]{:S(2)}) collective-permute-start(f32[2,256]{1,0:T(2,128)S(1)} %pad_maximum_fusion), channel_id=1, source_target_pairs={{4,0},{6,2},{0,4},{2,6},{5,1},{7,3},{1,5},{3,7},{12,8},{14,10},{8,... | collective-permute-start | bytes 6152 | tf_op jit(solution)/shard_map/ppermute | solution.py:16
  27.0 9.3 %copy-start.9 = (bf16[256,1280]{0,1:T(8,128)(2,1)}, bf16[256,1280]{0,1:T(8,128)(2,1)S(1)}, u32[]{:S(2)}) copy-start(bf16[256,1280]{0,1:T(8,128)(2,1)S(1)} %fusion.48) | copy-start | bytes 1966084
  27.3 8.5 %copy-start.3 = (bf16[256,1280]{0,1:T(8,128)(2,1)}, bf16[256,1280]{0,1:T(8,128)(2,1)S(1)}, u32[]{:S(2)}) copy-start(bf16[256,1280]{0,1:T(8,128)(2,1)S(1)} %fusion.40) | copy-start | bytes 1966084
  28.7 23.8 %collective-permute-start.3 = (bf16[256,1280]{0,1:T(8,128)(2,1)}, bf16[256,1280]{0,1:T(8,128)(2,1)}, u32[]{:S(2)}, u32[]{:S(2)}) collective-permute-start(bf16[256,1280]{0,1:T(8,128)(2,1)} %collective-permute-done.1), channel_id=1, source_target_pairs={{0,8},{8,16},{16,24},{24,0},{1,9},{9,17},{17,25},{25,1},{2,10},{10... | collective-permute-start | bytes 1966088 | tf_op jit(solution)/shard_map/ppermute | solution.py:93
  35.8 1.1 copy-start.7
  55.5 2.8 %copy-start.6 = (bf16[256,1280]{0,1:T(8,128)(2,1)S(1)}, bf16[256,1280]{0,1:T(8,128)(2,1)}, u32[]{:S(2)}) copy-start(bf16[256,1280]{0,1:T(8,128)(2,1)} %copy.52) | copy-start | bytes 1966084
  55.5 2.8 %copy-start.8 = (bf16[256,1280]{0,1:T(8,128)(2,1)S(1)}, bf16[256,1280]{0,1:T(8,128)(2,1)}, u32[]{:S(2)}) copy-start(bf16[256,1280]{0,1:T(8,128)(2,1)} %copy.42) | copy-start | bytes 1966084
  58.3 1.1 copy-start.10
  59.4 1.4 copy-start.4
  76.2 2.1 %copy-start.5 = (f32[10,128,256]{2,1,0:T(8,128)S(1)}, f32[10,128,256]{2,1,0:T(8,128)}, u32[]{:S(2)}) copy-start(f32[10,128,256]{2,1,0:T(8,128)} %convolution_multiply_fusion) | copy-start | bytes 3932164
  76.2 86.0 %copy-start.14 = (bf16[10,256,128]{1,2,0:T(8,128)(2,1)S(1)}, bf16[10,256,128]{1,2,0:T(8,128)(2,1)}, u32[]{:S(2)}) copy-start(bf16[10,256,128]{1,2,0:T(8,128)(2,1)} %get-tuple-element.438) | copy-start | bytes 1966084
  78.3 85.0 %copy-start.2 = (bf16[256,1280]{0,1:T(8,128)(2,1)S(1)}, bf16[256,1280]{0,1:T(8,128)(2,1)}, u32[]{:S(2)}) copy-start(bf16[256,1280]{0,1:T(8,128)(2,1)} %copy-done.1) | copy-start | bytes 1966084
  85.1 78.2 %collective-permute-start.4 = (f32[2,256]{1,0:T(2,128)S(1)}, f32[2,256]{1,0:T(2,128)S(1)}, u32[]{:S(2)}, u32[]{:S(2)}) collective-permute-start(f32[2,256]{1,0:T(2,128)S(1)} %pad_maximum_fusion.1), channel_id=1, source_target_pairs={{4,0},{6,2},{0,4},{2,6},{5,1},{7,3},{1,5},{3,7},{12,8},{14,10},{8,... | collective-permute-start | bytes 6152 | tf_op jit(solution)/shard_map/ppermute | solution.py:16
Sparse Core Ops, SparseCore 0:
  9.5 38.4 all-gather.2
  50.1 26.0 all-gather.4
